TPU v7x, 256 devices: a whole 4x4x8 slice. The times are simulated.
256 devices in a mesh: lat: 32 (over y_hi, z, core), lon: 8 (over y_lo, x).
Axes of the slice: x: 4, y: 4 (y_hi: 2, y_lo: 2; y = y_hi * 2 + y_lo), z: 8, core: 2. Of those that a mesh axis runs over, the one named last changes fastest.
Arguments:
- features: bfloat16 [512, 512, 512], P('lat', 'lon'), may hold values from -6 to 6
- upstream: bfloat16 [512, 512, 512], P('lat', 'lon'), may hold values from -6 to 6
- kernel: bfloat16 [4608, 512], replicated, may hold values from -0.09375 to 0.09375
Outputs:
- input_grad: bfloat16 [512, 512, 512], P('lat', 'lon')
- direction: float32 [4608, 512], P('lat')
- perturbed: float32 [4608, 512], P('lat')
All inputs are finite; a program needn't handle non-finite values.
Results may differ from a plain program's by a relative error of at most 0.0032.
Values may be sent and summed in bfloat16 or wider, within the bound.
A program may use at most 128 MiB of HBM per device.

v0:
```python
import jax
import jax.numpy as jnp
from jax import lax
from jax.sharding import PartitionSpec as P


def padded_2(block, sides, width, periodic):
    for axis, dim in sides:
        count = lax.axis_size(axis)
        forward = [(i, i + 1) for i in range(count - 1)]
        if periodic:
            forward.append((count - 1, 0))
        backward = [(target, source) for source, target in forward]
        low = lax.ppermute(
            lax.slice_in_dim(block, block.shape[dim] - width, None, axis=dim), axis, forward
        )
        high = lax.ppermute(lax.slice_in_dim(block, 0, width, axis=dim), axis, backward)
        block = jnp.concatenate([low, block, high], axis=dim)
    return block


def from_everyone(x, axis):
    size = lax.axis_size(axis)
    return lax.all_to_all(jnp.broadcast_to(x[None], (size, *x.shape)), axis, 0, 0, tiled=True)


def taken_together(x, axis):
    return from_everyone(x, axis).sum(axis=0)


def convolve(padded, kernel, height, breadth):
    channels = kernel.shape[1]
    total = jnp.zeros((height, breadth, channels), jnp.float32)
    for a in range(3):
        for b in range(3):
            t = 3 * a + b
            total = total + jnp.dot(
                padded[a : a + height, b : b + breadth],
                kernel[t * channels : (t + 1) * channels],
                preferred_element_type=jnp.float32,
            )
    return total


def spread(padded, kernel, height, breadth):
    channels = kernel.shape[1]
    total = jnp.zeros((height, breadth, channels), jnp.float32)
    for a in range(3):
        for b in range(3):
            t = 3 * a + b
            piece = padded[2 - a : 2 - a + height, 2 - b : 2 - b + breadth]
            total = total + lax.dot_general(
                piece,
                kernel[t * channels : (t + 1) * channels],
                (((2,), (1,)), ((), ())),
                preferred_element_type=jnp.float32,
            )
    return total


def weight_terms(padded, slope, height, breadth):
    blocks = []
    for a in range(3):
        for b in range(3):
            blocks.append(
                lax.dot_general(
                    padded[a : a + height, b : b + breadth],
                    slope,
                    (((0, 1), (0, 1)), ((), ())),
                    preferred_element_type=jnp.float32,
                )
            )
    return jnp.concatenate(blocks, axis=0)


def gated(upstream, z):
    sig = jax.nn.sigmoid(z)
    return upstream.astype(jnp.float32) * sig * (1.0 + z * (1.0 - sig))


def shards(features, upstream, kernel):
    height, breadth, channels = features.shape
    wide_cols = padded_2(features, (("lon", 1),), 1, True)
    padded_x = padded_2(wide_cols, (("lat", 0),), 1, False)
    z = convolve(padded_x, kernel, height, breadth)
    slope = gated(upstream, z).astype(jnp.bfloat16)
    slope_cols = padded_2(slope, (("lon", 1),), 1, True)
    padded_slope = padded_2(slope_cols, (("lat", 0),), 1, False)
    back = upstream.astype(jnp.float32) + spread(padded_slope, kernel, height, breadth)
    input_grad = back.astype(jnp.bfloat16)
    local_grad = weight_terms(padded_x, slope, height, breadth)
    row_block = lax.psum_scatter(local_grad, "lat", scatter_dimension=0, tiled=True)
    summed = taken_together(row_block, "lon")
    total = taken_together(jnp.sum(summed * summed), "lat")
    count = 9.0 * channels * channels
    direction = summed / jnp.sqrt(total / count + 1e-06)
    block_rows = summed.shape[0]
    start = lax.axis_index("lat") * block_rows
    own_kernel = lax.dynamic_slice_in_dim(kernel, start, block_rows, 0)
    perturbed = own_kernel.astype(jnp.float32) + 0.05 / jnp.sqrt(count) * direction
    return (input_grad, direction, perturbed)


def solution(mesh):
    return jax.shard_map(
        shards,
        mesh=mesh,
        in_specs=(P("lat", "lon", None), P("lat", "lon", None), P()),
        out_specs=(P("lat", "lon", None), P("lat", None), P("lat", None)),
        check_vma=False,
    )
```

profile of v0, /device:TPU:1, one launch (start us, length us, event | category | flops | bytes accessed | tf_op | source)
XLA Modules:
  0.0 273.2 jit_solution(1430454105132169985)
XLA Ops:
  8.3 2.1 collective-permute-start
  10.4 2.4 collective-permute-start.1
  12.8 2.1 fusion.62
  15.0 4.9 %collective-permute-start.2 = (bf16[1,66,512]{2,1,0:T(8,128)(2,1)S(1)}, bf16[1,66,512]{2,1,0:T(8,128)(2,1)S(1)}, u32[]{:S(2)}, u32[]{:S(2)}) collective-permute-start(bf16[1,66,512]{2,1,0:T(8,128)(2,1)S(1)} %get-tuple-element.11), channel_id=1, source_target_pairs={{0,8},{8,16},{16,24},{24,32},{32,40},{40,48},{48,56},{56,64},{64,7... | collective-permute-start | bytes 202760 | tf_op jit(solution)/shard_map/ppermute | solution.py:14
  19.9 2.1 collective-permute-start.3
  22.0 1.8 fusion.50
  30.4 1.9 fusion.1
  37.5 1.8 fusion.8
  39.2 1.7 fusion.7
  41.0 1.8 fusion.6
  42.7 1.7 fusion.5
  44.5 1.8 fusion.4
  46.3 1.8 fusion.3
  48.2 3.7 %collective-permute-start.5 = (bf16[16,1,512]{2,1,0:T(2,128)(2,1)S(1)}, bf16[16,1,512]{2,1,0:T(2,128)(2,1)S(1)}, u32[]{:S(2)}, u32[]{:S(2)}) collective-permute-start(bf16[16,1,512]{2,1,0:T(2,128)(2,1)S(1)} %get-tuple-element.14), channel_id=1, source_target_pairs={{1,0},{2,1},{3,2},{4,3},{5,4},{6,5},{7,6},{0,7},{9,8},{10,9},{11,1... | collective-permute-start | bytes 49160 | tf_op jit(solution)/shard_map/ppermute | solution.py:17
  51.9 3.1 %fusion.60 = f32[16,64,512]{2,1,0:T(8,128)} fusion(bf16[16,64,512]{2,1,0:T(8,128)(2,1)S(1)} %fusion.1, bf16[4608,512]{1,0:T(8,128)(2,1)} %param.5), kind=kOutput, calls=%fused_computation.75 | convolution fusion | flops 536870912 | bytes 3670016 | tf_op jit(solution)/shard_map/dot_general | solution.py:52
  55.0 1.8 collective-permute-done.4
  57.4 1.9 collective-permute-start.6
  59.4 4.3 %collective-permute-start.7 = (bf16[1,66,512]{2,1,0:T(8,128)(2,1)S(1)}, bf16[1,66,512]{2,1,0:T(8,128)(2,1)}, u32[]{:S(2)}, u32[]{:S(2)}) collective-permute-start(bf16[1,66,512]{2,1,0:T(8,128)(2,1)S(1)} %get-tuple-element.8), channel_id=1, source_target_pairs={{0,8},{8,16},{16,24},{24,32},{32,40},{40,48},{48,56},{56,64},{64,7... | collective-permute-start | bytes 202760 | tf_op jit(solution)/shard_map/ppermute | solution.py:14
  63.6 3.2 %fusion.22 = f32[16,64,512]{2,1,0:T(8,128)} fusion(bf16[16,1,512]{2,1,0:T(2,128)(2,1)S(1)} %collective-permute-done.5, bf16[16,64,512]{2,1,0:T(8,128)(2,1)S(1)} %fusion.1, bf16[4608,512]{1,0:T(8,128)(2,1)} %param.5), kind=kOutput, calls=%fused_computation.37 | convolution fusion | flops 538968064 | bytes 3686400 | tf_op jit(solution)/shard_map/dot_general | solution.py:52
  66.9 138.9 %reduce-scatter.2.cloned.1.call-done = f32[144,512]{1,0:T(8,128)} async-done(((f32[4608,512]{1,0:T(8,128)}), f32[144,512]{1,0:T(8,128)}) %reduce-scatter.2.cloned.1.call-update) | async-done | bytes 294928 | tf_op jit(solution)/shard_map/reduce_scatter | solution.py:92
  205.8 2.7 broadcast_in_dim.4
  208.5 4.0 %all-to-all-start = ((f32[8,144,512]{2,1,0:T(8,128)}), f32[8,144,512]{2,1,0:T(8,128)S(1)}, u32[]{:S(2)}, u32[]{:S(2)}) async-start(f32[8,144,512]{2,1,0:T(8,128)} %broadcast_in_dim.4), calls=%async_computation.1 | async-start | bytes 4718592 | tf_op jit(solution)/shard_map/all_to_all | solution.py:24
  212.4 3.1 %fusion.20 = f32[16,64,512]{2,1,0:T(8,128)} fusion(bf16[16,64,512]{2,1,0:T(8,128)(2,1)S(1)} %fusion.1, bf16[16,1,512]{2,1,0:T(2,128)(2,1)S(1)} %collective-permute-done.4, bf16[4608,512]{1,0:T(8,128)(2,1)} %param.5), kind=kOutput, calls=%fused_computation.34 | convolution fusion | flops 538968064 | bytes 3686400 | tf_op jit(solution)/shard_map/dot_general | solution.py:52
  217.2 3.5 %fusion.16 = f32[16,64,512]{2,1,0:T(8,128)} fusion(bf16[17,66,512]{2,1,0:T(8,128)(2,1)S(1)} %get-tuple-element.6, bf16[4608,512]{1,0:T(8,128)(2,1)} %param.5), kind=kOutput, calls=%fused_computation.29 | convolution fusion | flops 536870912 | bytes 3670016 | tf_op jit(solution)/shard_map/dot_general | solution.py:52
  220.8 3.2 %fusion.18 = f32[16,64,512]{2,1,0:T(8,128)} fusion(bf16[17,66,512]{2,1,0:T(8,128)(2,1)S(1)} %get-tuple-element.6, bf16[4608,512]{1,0:T(8,128)(2,1)} %param.5), kind=kOutput, calls=%fused_computation.31 | convolution fusion | flops 536870912 | bytes 3670016 | tf_op jit(solution)/shard_map/dot_general | solution.py:52
  223.9 3.1 %fusion.24 = f32[16,64,512]{2,1,0:T(8,128)} fusion(bf16[17,66,512]{2,1,0:T(8,128)(2,1)S(1)} %get-tuple-element.5, bf16[4608,512]{1,0:T(8,128)(2,1)} %param.5), kind=kOutput, calls=%fused_computation.39 | convolution fusion | flops 536870912 | bytes 3670016 | tf_op jit(solution)/shard_map/dot_general | solution.py:52
  227.0 3.1 %fusion.26 = f32[16,64,512]{2,1,0:T(8,128)} fusion(bf16[17,66,512]{2,1,0:T(8,128)(2,1)S(1)} %get-tuple-element.5, bf16[4608,512]{1,0:T(8,128)(2,1)} %param.5), kind=kOutput, calls=%fused_computation.41 | convolution fusion | flops 536870912 | bytes 3670016 | tf_op jit(solution)/shard_map/dot_general | solution.py:52
  230.1 3.1 %fusion.28 = f32[16,64,512]{2,1,0:T(8,128)} fusion(bf16[17,66,512]{2,1,0:T(8,128)(2,1)S(1)} %get-tuple-element.5, bf16[4608,512]{1,0:T(8,128)(2,1)} %param.5), kind=kOutput, calls=%fused_computation.43 | convolution fusion | flops 536870912 | bytes 3670016 | tf_op jit(solution)/shard_map/dot_general | solution.py:52
  233.3 9.0 %all-to-all-done = f32[8,144,512]{2,1,0:T(8,128)S(1)} async-done(((f32[8,144,512]{2,1,0:T(8,128)}), f32[8,144,512]{2,1,0:T(8,128)S(1)}, u32[]{:S(2)}, u32[]{:S(2)}) %all-to-all-start) | async-done | bytes 2359328 | tf_op jit(solution)/shard_map/all_to_all | solution.py:24
  246.1 7.8 %all-to-all-start.1 = ((f32[32,1,1]{2,1,0:T(1,128)}), f32[32,1,1]{2,1,0:T(1,128)S(1)}, u32[]{:S(2)}, u32[]{:S(2)}) async-start(f32[32,1,1]{2,1,0:T(1,128)} %broadcast_in_dim.5), calls=%async_computation.2 | async-start | bytes 32768 | tf_op jit(solution)/shard_map/all_to_all | solution.py:24
  254.0 8.6 %fusion.2 = bf16[16,64,512]{2,1,0:T(8,128)(2,1)} fusion(bf16[16,64,512]{2,1,0:T(8,128)(2,1)S(1)} %copy-done.3, f32[16,64,512]{2,1,0:T(8,128)} %fusion.16, f32[16,64,512]{2,1,0:T(8,128)} %fusion.18, f32[16,64,512]{2,1,0:T(8,128)} %fusion.20, f32[16,64,512]{2,1,0:T(8,128)} %fusion.60, f32[16,64,512]{2,1,0:T(8,128)} %fusion.22, f32[16,64,512]{2,1,0:T(8,128)} %fusion.24, ...), kind=kOutput, calls=%fused_computation.4 | convolution fusion | flops 542638080 | bytes 20447232 | tf_op jit(solution)/shard_map/dot_general | solution.py:52
  264.6 1.8 multiply_add_fusion
  (42 shorter events, 20.5 us)
Async XLA Ops:
  7.2 7.7 %copy-start = (bf16[16,64,512]{2,1,0:T(8,128)(2,1)S(1)}, bf16[16,64,512]{2,1,0:T(8,128)(2,1)}, u32[]{:S(2)}) copy-start(bf16[16,64,512]{2,1,0:T(8,128)(2,1)} %param.3) | copy-start | bytes 3145732
  7.2 198.6 %reduce-scatter.2.cloned.1.call-start = ((), (), s32[]{:S(2)}) async-start(), calls=%async_computation.3 | async-start | bytes 9732096 | tf_op jit(solution)/shard_map/reduce_scatter | solution.py:92
  8.3 6.5 %collective-permute-start = (bf16[16,1,512]{2,1,0:T(2,128)(2,1)S(1)}, bf16[16,1,512]{2,1,0:T(2,128)(2,1)S(1)}, u32[]{:S(2)}, u32[]{:S(2)}) collective-permute-start(bf16[16,1,512]{2,1,0:T(2,128)(2,1)S(1)} %get-tuple-element.15), channel_id=1, source_target_pairs={{0,1},{1,2},{2,3},{3,4},{4,5},{5,6},{6,7},{7,0},{8,9},{9,10},{10,1... | collective-permute-start | bytes 49160 | tf_op jit(solution)/shard_map/ppermute | solution.py:14
  10.4 4.4 %collective-permute-start.1 = (bf16[16,1,512]{2,1,0:T(2,128)(2,1)S(1)}, bf16[16,1,512]{2,1,0:T(2,128)(2,1)S(1)}, u32[]{:S(2)}, u32[]{:S(2)}) collective-permute-start(bf16[16,1,512]{2,1,0:T(2,128)(2,1)S(1)} %get-tuple-element.16), channel_id=1, source_target_pairs={{1,0},{2,1},{3,2},{4,3},{5,4},{6,5},{7,6},{0,7},{9,8},{10,9},{11,1... | collective-permute-start | bytes 49160 | tf_op jit(solution)/shard_map/ppermute | solution.py:17
  14.9 8.9 %copy-start.4 = (bf16[4608,512]{1,0:T(8,128)(2,1)S(1)}, bf16[4608,512]{1,0:T(8,128)(2,1)}, u32[]{:S(2)}) copy-start(bf16[4608,512]{1,0:T(8,128)(2,1)} %param.5) | copy-start | bytes 14155780
  15.0 9.6 %collective-permute-start.2 = (bf16[1,66,512]{2,1,0:T(8,128)(2,1)S(1)}, bf16[1,66,512]{2,1,0:T(8,128)(2,1)S(1)}, u32[]{:S(2)}, u32[]{:S(2)}) collective-permute-start(bf16[1,66,512]{2,1,0:T(8,128)(2,1)S(1)} %get-tuple-element.11), channel_id=1, source_target_pairs={{0,8},{8,16},{16,24},{24,32},{32,40},{40,48},{48,56},{56,64},{64,7... | collective-permute-start | bytes 202760 | tf_op jit(solution)/shard_map/ppermute | solution.py:14
  19.9 5.7 %collective-permute-start.3 = (bf16[1,66,512]{2,1,0:T(8,128)(2,1)S(1)}, bf16[1,66,512]{2,1,0:T(8,128)(2,1)S(1)}, u32[]{:S(2)}, u32[]{:S(2)}) collective-permute-start(bf16[1,66,512]{2,1,0:T(8,128)(2,1)S(1)} %get-tuple-element.12), channel_id=1, source_target_pairs={{8,0},{16,8},{24,16},{32,24},{40,32},{48,40},{56,48},{64,56},{72,6... | collective-permute-start | bytes 202760 | tf_op jit(solution)/shard_map/ppermute | solution.py:17
  29.2 1.2 copy-start.2
  48.2 6.8 %collective-permute-start.5 = (bf16[16,1,512]{2,1,0:T(2,128)(2,1)S(1)}, bf16[16,1,512]{2,1,0:T(2,128)(2,1)S(1)}, u32[]{:S(2)}, u32[]{:S(2)}) collective-permute-start(bf16[16,1,512]{2,1,0:T(2,128)(2,1)S(1)} %get-tuple-element.14), channel_id=1, source_target_pairs={{1,0},{2,1},{3,2},{4,3},{5,4},{6,5},{7,6},{0,7},{9,8},{10,9},{11,1... | collective-permute-start | bytes 49160 | tf_op jit(solution)/shard_map/ppermute | solution.py:17
  51.9 4.9 %collective-permute-start.4 = (bf16[16,1,512]{2,1,0:T(2,128)(2,1)S(1)}, bf16[16,1,512]{2,1,0:T(2,128)(2,1)S(1)}, u32[]{:S(2)}, u32[]{:S(2)}) collective-permute-start(bf16[16,1,512]{2,1,0:T(2,128)(2,1)S(1)} %get-tuple-element.13), channel_id=1, source_target_pairs={{0,1},{1,2},{2,3},{3,4},{4,5},{5,6},{6,7},{7,0},{8,9},{9,10},{10,1... | collective-permute-start | bytes 49160 | tf_op jit(solution)/shard_map/ppermute | solution.py:14
  57.4 158.1 %collective-permute-start.6 = (bf16[1,66,512]{2,1,0:T(8,128)(2,1)}, bf16[1,66,512]{2,1,0:T(8,128)(2,1)}, u32[]{:S(2)}, u32[]{:S(2)}) collective-permute-start(bf16[1,66,512]{2,1,0:T(8,128)(2,1)} %get-tuple-element.7), channel_id=1, source_target_pairs={{8,0},{16,8},{24,16},{32,24},{40,32},{48,40},{56,48},{64,56},{72,6... | collective-permute-start | bytes 202760 | tf_op jit(solution)/shard_map/ppermute | solution.py:17
  59.4 156.2 %collective-permute-start.7 = (bf16[1,66,512]{2,1,0:T(8,128)(2,1)S(1)}, bf16[1,66,512]{2,1,0:T(8,128)(2,1)}, u32[]{:S(2)}, u32[]{:S(2)}) collective-permute-start(bf16[1,66,512]{2,1,0:T(8,128)(2,1)S(1)} %get-tuple-element.8), channel_id=1, source_target_pairs={{0,8},{8,16},{16,24},{24,32},{32,40},{40,48},{48,56},{56,64},{64,7... | collective-permute-start | bytes 202760 | tf_op jit(solution)/shard_map/ppermute | solution.py:14
  208.5 33.7 %all-to-all-start = ((f32[8,144,512]{2,1,0:T(8,128)}), f32[8,144,512]{2,1,0:T(8,128)S(1)}, u32[]{:S(2)}, u32[]{:S(2)}) async-start(f32[8,144,512]{2,1,0:T(8,128)} %broadcast_in_dim.4), calls=%async_computation.1 | async-start | bytes 4718592 | tf_op jit(solution)/shard_map/all_to_all | solution.py:24
  217.2 6.7 %copy-start.1 = (bf16[17,66,512]{2,1,0:T(8,128)(2,1)}, bf16[17,66,512]{2,1,0:T(8,128)(2,1)S(1)}, u32[]{:S(2)}) copy-start(bf16[17,66,512]{2,1,0:T(8,128)(2,1)S(1)} %get-tuple-element.6) | copy-start | bytes 3446788
  233.3 20.7 %copy-start.3 = (bf16[16,64,512]{2,1,0:T(8,128)(2,1)S(1)}, bf16[16,64,512]{2,1,0:T(8,128)(2,1)}, u32[]{:S(2)}) copy-start(bf16[16,64,512]{2,1,0:T(8,128)(2,1)} %param.4) | copy-start | bytes 3145732
  246.1 17.1 %all-to-all-start.1 = ((f32[32,1,1]{2,1,0:T(1,128)}), f32[32,1,1]{2,1,0:T(1,128)S(1)}, u32[]{:S(2)}, u32[]{:S(2)}) async-start(f32[32,1,1]{2,1,0:T(1,128)} %broadcast_in_dim.5), calls=%async_computation.2 | async-start | bytes 32768 | tf_op jit(solution)/shard_map/all_to_all | solution.py:24
  253.9 10.6 %copy-start.5 = (f32[144,512]{1,0:T(8,128)S(1)}, f32[144,512]{1,0:T(8,128)}, u32[]{:S(2)}) copy-start(f32[144,512]{1,0:T(8,128)} %reduce_sum.27) | copy-start | bytes 884740
Sparse Core Ops, SparseCore 0:
  48.2 157.5 reduce-scatter.1
where the time goes:
time: 274 us; the launch traced here: 273 us
  waiting for transfers between devices  151 us (55%)
  matrix products  59.8 us (22%)
  starting transfers between devices  33.3 us (12%)
  between operations  14.9 us (5%)
  other arithmetic  8.16 us (3%)
  local copies, waits for them, and re-layouts  5.66 us (2%)
    reduce_scatter x1, waiting for transfers between devices, shards(): lax.psum_scatter(local_grad, 'lat', scatter_dimension=0, tiled=True)  139 us
    dot_general x9, matrix products, spread(): lax.dot_general(piece, kernel[t * channels:(t + 1) * channels], (((2,), (...  34.1 us
    dot_general x9, matrix products, weight_terms(): lax.dot_general(padded[a:a + height, b:b + breadth], slope, (((0, 1), (0,...  15.7 us
    all_to_all x2, starting transfers between devices, from_everyone(): lax.all_to_all(jnp.broadcast_to(x[None], (size, *x.shape)), axis, 0, 0, t...  11.8 us
    ppermute x4, starting transfers between devices, padded_2(): lax.ppermute(lax.slice_in_dim(block, block.shape[dim] - width, None, axis...  11.3 us
    ppermute x4, starting transfers between devices, padded_2(): lax.ppermute(lax.slice_in_dim(block, 0, width, axis=dim), axis, backward)  10.1 us
    dot_general x9, matrix products, convolve(): jnp.dot(padded[a:a + height, b:b + breadth], kernel[t * channels:(t + 1)...  10 us
    all_to_all x2, waiting for transfers between devices, from_everyone(): lax.all_to_all(jnp.broadcast_to(x[None], (size, *x.shape)), axis, 0, 0, t...  9.65 us
  transfers between devices with their start and end apart: 11, of which 5 were waited for; matrix products, arithmetic and copies ran while one was open for 16% of the time, Pallas kernels for 0%

commit v1 on v0

v1 whole, which is shorter than its diff:
```python
import functools

import jax
import jax.numpy as jnp
from jax import lax
from jax.experimental import pallas as pl
from jax.experimental.pallas import tpu as pltpu
from jax.sharding import PartitionSpec as P

MESH = pl.DeviceIdType.MESH
F32, BF16 = jnp.float32, jnp.bfloat16

H, W, C = 16, 64, 512
POS = H * W
YHI, ZN, LON, LAT = 2, 8, 8, 32
PR, PC = 72, 128
BLOCK = 144

ORDERS = (
    (("x", "A"), ("x", "B"), ("y", "A"), ("y", "B")),
    (("y", "A"), ("y", "B"), ("x", "A"), ("x", "B")),
    (("x", "B"), ("x", "A"), ("y", "B"), ("y", "A")),
    (("y", "B"), ("y", "A"), ("x", "B"), ("x", "A")),
)
GROUPS = (
    (((0, 0), (0, 384), (0, 768)), ((1, 768), (1, 1152), (2, 0))),
    (((0, 1152), (1, 0), (1, 384)), ((2, 384), (2, 768), (2, 1152))),
)


def flip(p):
    return p + 1 - 2 * (p % 2)


def gated(upstream, z):
    sig = jax.nn.sigmoid(z)
    return upstream.astype(F32) * sig * (1.0 + z * (1.0 - sig))


def kernel(
    x_hbm, u_hbm, k_hbm, ig_hbm, dir_hbm, per_hbm,
    x_v, u_v, k_v, x3, s3, s_v, ig_v, dir_v, per_v,
    colx, hrowx, hcolx, hcorx, cols, hrows, hcols, hcors,
    acc, csend, crecv, send1, send2, send3, send4, recv1, recv2, recv3, recv4,
    pieces, zsend, zrecv, ag, norms,
    lsem, hsx, hrx, hss, hrs, cs_sem, cr_sem, ss_sem, sr_sem, zs_sem, zr_sem, as_sem, ar_sem, ns_sem, nr_sem,
):
    lat, lon = lax.axis_index("lat"), lax.axis_index("lon")
    core, zc, yhi = lat % 2, (lat // 2) % 8, lat // 16
    xc, ylo = lon % 4, lon // 4
    yc = 2 * yhi + ylo

    def place(yy, zz, cc, xx):
        return ((yy // 2) * 16 + zz * 2 + cc, (yy % 2) * 4 + xx)

    def x_peer(q):
        return place(yc, zc, core, q)

    def y_peer(q):
        return place(q, zc, core, xc)

    def z_peer(q):
        return place(yc, q, core, xc)

    up, down = (lat + LAT - 1) % LAT, (lat + 1) % LAT
    left, right = (lon + LON - 1) % LON, (lon + 1) % LON

    loads = [
        pltpu.make_async_copy(src, dst, lsem.at[i])
        for i, (src, dst) in enumerate(((x_hbm, x_v), (k_hbm, k_v), (u_hbm, u_v)))
    ]
    for load in loads:
        load.start()

    barrier = pltpu.get_barrier_semaphore()
    greeted = [
        (up, lon), (down, lon), (lat, left), (lat, right),
        (up, left), (up, right), (down, left), (down, right),
        x_peer(flip(xc)), x_peer(3 - xc), y_peer(flip(yc)), y_peer(3 - yc),
    ] + [z_peer((zc + d) % ZN) for d in range(1, ZN)]
    for peer in greeted:
        pl.semaphore_signal(barrier, inc=1, device_id=peer, device_id_type=MESH)

    def remote(src, dst, ssem, rsem, peer):
        return pltpu.make_async_remote_copy(
            src_ref=src, dst_ref=dst, send_sem=ssem, recv_sem=rsem, device_id=peer, device_id_type=MESH
        )

    def edge_columns(src, col):
        def body(h, carry):
            base = pl.multiple_of(h * W, W)
            col[0, pl.ds(h, 1), :] = src[pl.ds(base, 16), :].astype(F32)[0:1]
            col[1, pl.ds(h, 1), :] = src[pl.ds(base + W - 16, 16), :].astype(F32)[15:16]
            return carry
        lax.fori_loop(0, H, body, 0)

    def halo(src, col, hrow, hcol, hcor, ssem, rsem):
        plan = (
            (src.at[pl.ds((H - 1) * W, W)], hrow.at[0], (down, lon)),
            (src.at[pl.ds(0, W)], hrow.at[1], (up, lon)),
            (col.at[1], hcol.at[0], (lat, right)),
            (col.at[0], hcol.at[1], (lat, left)),
            (col.at[1, pl.ds(8, 8)], hcor.at[0], (down, right)),
            (col.at[0, pl.ds(8, 8)], hcor.at[1], (down, left)),
            (col.at[1, pl.ds(0, 8)], hcor.at[2], (up, right)),
            (col.at[0, pl.ds(0, 8)], hcor.at[3], (up, left)),
        )
        return [remote(a, b, ssem.at[i], rsem.at[i], peer) for i, (a, b, peer) in enumerate(plan)]

    rows = lax.broadcasted_iota(jnp.int32, (W, C), 0)
    above = jnp.where(lat == 0, 0.0, 1.0).astype(F32)
    below = jnp.where(lat == LAT - 1, 0.0, 1.0).astype(F32)

    def shifted(dst, base, row, low, high):
        dst[pl.ds(base, W), C : 2 * C] = row.astype(BF16)
        dst[pl.ds(base, W), 0:C] = jnp.where(rows == 0, low, pltpu.roll(row, 1, 0)).astype(BF16)
        dst[pl.ds(base, W), 2 * C : 3 * C] = jnp.where(rows == W - 1, high, pltpu.roll(row, W - 1, 0)).astype(BF16)

    def build(src, hrow, hcol, hcor, dst):
        def body(h, carry):
            base = pl.multiple_of(h * W, W)
            shifted(
                dst, pl.multiple_of(base + W, W), src[pl.ds(base, W), :].astype(F32),
                hcol[0, pl.ds(h, 1), :], hcol[1, pl.ds(h, 1), :],
            )
            return carry
        lax.fori_loop(0, H, body, 0)
        shifted(dst, 0, hrow[0].astype(F32) * above, hcor[0, 7:8, :] * above, hcor[1, 7:8, :] * above)
        shifted(
            dst, (H + 1) * W, hrow[1].astype(F32) * below, hcor[2, 0:1, :] * below, hcor[3, 0:1, :] * below
        )

    loads[0].wait()
    edge_columns(x_v, colx)
    pl.semaphore_wait(barrier, len(greeted))
    halo_x = halo(x_v, colx, hrowx, hcolx, hcorx, hsx, hrx)
    for copy in halo_x:
        copy.start()
    loads[1].wait()
    loads[2].wait()
    for copy in halo_x:
        copy.wait_recv()
    build(x_v, hrowx, hcolx, hcorx, x3)

    for c in range(4):
        z = jnp.zeros((256, C), F32)
        for a in range(3):
            z = z + jnp.dot(
                x3[(4 * c + a) * W : (4 * c + a) * W + 256, :],
                k_v[a * 3 * C : (a + 1) * 3 * C, :],
                preferred_element_type=F32,
            )
        s_v[256 * c : 256 * (c + 1), :] = gated(u_v[256 * c : 256 * (c + 1), :], z).astype(BF16)

    edge_columns(s_v, cols)
    halo_s = halo(s_v, cols, hrows, hcols, hcors, hss, hrs)
    for copy in halo_s:
        copy.start()

    partner = (flip(lat), lon)
    core_copies = [
        remote(csend.at[u], crecv.at[u], cs_sem.at[u], cr_sem.at[u], partner) for u in range(8)
    ]

    def weight_group(j):
        for hi in range(2):
            for m, (a, first) in enumerate(GROUPS[j][hi]):
                part = lax.dot_general(
                    x3[a * W : a * W + POS, first : first + 384],
                    s_v[...],
                    (((0,), (0,)), ((), ())),
                    preferred_element_type=F32,
                )
                row = 384 * m
                while row < 384 * (m + 1):
                    stop = min(384 * (m + 1), (row // PR + 1) * PR)
                    p = row // PR
                    zl, cc, lo = p // 4, (p // 2) % 2, p % 2
                    for xt in range(4):
                        acc[cc, 4 * j + zl, 2 * hi + lo, xt, row % PR : row % PR + stop - row, :] = part[
                            row - 384 * m : stop - 384 * m, PC * xt : PC * (xt + 1)
                        ]
                    row = stop
        for zl in range(4):
            u = 4 * j + zl
            for yy in range(4):
                for xx in range(4):
                    csend[u, 4 * yy + xx] = acc[1 - core, u, yy, xx].astype(BF16)
            core_copies[u].start()

    weight_group(0)
    weight_group(1)

    sends, recvs = (send1, send2, send3, send4), (recv1, recv2, recv3, recv4)

    def halves(kind, first, p):
        q = flip(p) if kind == "A" else 3 - p
        if first:
            other = (lambda c: 3 - c) if kind == "A" else flip
            return q, [(q, q), (other(q), other(q))], [(p, p), (other(p), other(p))]
        return q, [(q, 1)], [(p, 0)]

    started = {}

    def lists_after(u, steps):
        ys = [(i, i) for i in range(4)]
        xs = [(i, i) for i in range(4)]
        for s in range(steps):
            dim, kind = ORDERS[u % 4][s]
            _, _, keep = halves(kind, s % 2 == 0, xc if dim == "x" else yc)
            kept = [(v, i) for i, (v, _) in enumerate(keep)]
            if dim == "x":
                xs = kept
            else:
                ys = kept
        return ys, xs

    def advance(u, s):
        ys, xs = lists_after(u, s)
        if s == 0:
            core_copies[u].wait_recv()
            arrived = crecv
        else:
            started[u, s - 1].wait_recv()
            arrived = recvs[s - 1]
        wide = len(xs)
        dim, kind = ORDERS[u % 4][s]
        q, out, keep = halves(kind, s % 2 == 0, xc if dim == "x" else yc)
        send_y, send_x = (ys, out) if dim == "x" else (out, xs)
        keep_y, keep_x = (ys, keep) if dim == "x" else (keep, xs)
        slot = 0
        for yv, yi in send_y:
            for xv, xi in send_x:
                total = acc[core, u, yv, xv] + arrived[u, yi * wide + xi].astype(F32)
                sends[s][u, slot] = total.astype(BF16)
                slot += 1
        copy = remote(
            sends[s].at[u], recvs[s].at[u], ss_sem.at[s, u], sr_sem.at[s, u],
            x_peer(q) if dim == "x" else y_peer(q),
        )
        copy.start()
        started[u, s] = copy
        for yv, yi in keep_y:
            for xv, xi in keep_x:
                acc[core, u, yv, xv] = acc[core, u, yv, xv] + arrived[u, yi * wide + xi].astype(F32)

    def z_copy(u):
        return remote(zsend.at[u], zrecv.at[zc], zs_sem.at[u], zr_sem.at[zc], z_peer(u))

    def to_z(u):
        started[u, 3].wait_recv()
        total = acc[core, u, yc, xc] + recv4[u, 0].astype(F32)
        pieces[u] = total
        zsend[u] = total.astype(BF16)

        @pl.when(zc != u)
        def _():
            z_copy(u).start()

    def input_grad(c):
        n = 512
        total = u_v[n * c : n * (c + 1), :].astype(F32)
        grads = jnp.zeros((n, C), F32)
        for a in range(3):
            for b in range(3):
                t = 3 * a + b
                top = (8 * c + 2 - a) * W
                grads = grads + lax.dot_general(
                    s3[top : top + n, (2 - b) * C : (3 - b) * C],
                    k_v[t * C : (t + 1) * C, :],
                    (((1,), (1,)), ((), ())),
                    preferred_element_type=F32,
                )
        ig_v[n * c : n * (c + 1), :] = (total + grads).astype(BF16)

    first, second = range(4), range(4, 8)
    for u in first:
        advance(u, 0)
    for copy in halo_s:
        copy.wait_recv()
    build(s_v, hrows, hcols, hcors, s3)
    for u in second:
        advance(u, 0)
    input_grad(0)
    for u in first:
        advance(u, 1)
    input_grad(1)
    ig_copy = pltpu.make_async_copy(ig_v, ig_hbm, lsem.at[3])
    ig_copy.start()
    for u in second:
        advance(u, 1)
    for u in first:
        advance(u, 2)
    for u in second:
        advance(u, 2)
    for u in first:
        advance(u, 3)
    for u in second:
        advance(u, 3)
    for u in range(8):
        to_z(u)

    total = pieces[zc]
    for d in range(1, ZN):
        src = (zc + d) % ZN
        remote(zsend.at[0], zrecv.at[src], zs_sem.at[0], zr_sem.at[src], z_peer(src)).wait_recv()
        total = total + zrecv[src].astype(F32)

    ag[lon] = total
    ag_copies = []
    for d in range(1, LON):
        copy = remote(ag.at[lon], ag.at[lon], as_sem.at[d], ar_sem.at[lon], (lat, (lon + d) % LON))
        copy.start()
        ag_copies.append(copy)
    for d in range(1, LON):
        src = (lon + d) % LON
        remote(ag.at[src], ag.at[src], as_sem.at[0], ar_sem.at[src], (lat, src)).wait_recv()

    squares = jnp.zeros((PR, PC), F32)
    for i in range(LON):
        squares = squares + ag[i] * ag[i]
    norms[lat] = jnp.sum(squares, axis=0, keepdims=True)

    def norm_copy(d):
        return remote(
            norms.at[lat], norms.at[lat], ns_sem.at[d], nr_sem.at[lat], ((lat + d) % LAT, lon)
        )

    def norm_start(d, carry):
        norm_copy(d).start()
        return carry

    def norm_wait(d, carry):
        src = (lat + d) % LAT
        remote(norms.at[src], norms.at[src], ns_sem.at[d], nr_sem.at[src], (src, lon)).wait_recv()
        return carry

    lax.fori_loop(1, LAT, norm_start, 0)
    lax.fori_loop(1, LAT, norm_wait, 0)
    summed = jnp.sum(jnp.sum(norms[...], axis=0), axis=1, keepdims=True)
    count = 9.0 * C * C
    inverse = 1.0 / jnp.sqrt(summed / count + 1e-06)
    step = 0.05 / (count ** 0.5)
    own = k_v[pl.ds(pl.multiple_of(lat * BLOCK, 16), BLOCK), :].astype(F32)
    for i in range(LON):
        r0, c0 = (i // 4) * PR, (i % 4) * PC
        piece = ag[i] * inverse
        dir_v[r0 : r0 + PR, c0 : c0 + PC] = piece
        per_v[r0 : r0 + PR, c0 : c0 + PC] = own[r0 : r0 + PR, c0 : c0 + PC] + step * piece
    outs = [
        pltpu.make_async_copy(dir_v, dir_hbm, lsem.at[0]),
        pltpu.make_async_copy(per_v, per_hbm, lsem.at[1]),
    ]
    for copy in outs:
        copy.start()

    for copy in halo_x + halo_s + core_copies + list(started.values()) + ag_copies:
        copy.wait_send()
    for u in range(8):
        @pl.when(zc != u)
        def _():
            z_copy(u).wait_send()

    def norm_sent(d, carry):
        norm_copy(d).wait_send()
        return carry

    lax.fori_loop(1, LAT, norm_sent, 0)
    for copy in outs + [ig_copy]:
        copy.wait()


def shards(features, upstream, weights):
    any_spec = pl.BlockSpec(memory_space=pl.ANY)
    vmem = pltpu.VMEM
    dma = pltpu.SemaphoreType.DMA
    scratch = [
        vmem((POS, C), BF16), vmem((POS, C), BF16), vmem((9 * C, C), BF16),
        vmem(((H + 2) * W, 3 * C), BF16), vmem(((H + 2) * W, 3 * C), BF16), vmem((POS, C), BF16),
        vmem((POS, C), BF16), vmem((BLOCK, C), F32), vmem((BLOCK, C), F32),
    ]
    for _ in range(2):
        scratch += [vmem((2, H, C), F32), vmem((2, W, C), BF16), vmem((2, H, C), F32), vmem((4, 8, C), F32)]
    scratch += [vmem((2, 8, 4, 4, PR, PC), F32), vmem((8, 16, PR, PC), BF16), vmem((8, 16, PR, PC), BF16)]
    scratch += [vmem((8, n, PR, PC), BF16) for n in (8, 4, 2, 1)] * 2
    scratch += [
        vmem((8, PR, PC), F32), vmem((8, PR, PC), BF16), vmem((8, PR, PC), BF16),
        vmem((LON, PR, PC), F32), vmem((LAT, 1, PC), F32),
        dma((4,)), dma((8,)), dma((8,)), dma((8,)), dma((8,)), dma((8,)), dma((8,)),
        dma((4, 8)), dma((4, 8)), dma((8,)), dma((8,)), dma((8,)), dma((8,)), dma((LAT,)), dma((LAT,)),
    ]
    grad, direction, perturbed = pl.pallas_call(
        kernel,
        name="ascent",
        out_shape=(
            jax.ShapeDtypeStruct((POS, C), BF16),
            jax.ShapeDtypeStruct((BLOCK, C), F32),
            jax.ShapeDtypeStruct((BLOCK, C), F32),
        ),
        in_specs=[any_spec] * 3,
        out_specs=(any_spec,) * 3,
        scratch_shapes=scratch,
        compiler_params=pltpu.CompilerParams(
            collective_id=0, has_side_effects=True, vmem_limit_bytes=62 * 1024 * 1024
        ),
    )(features.reshape(POS, C), upstream.reshape(POS, C), weights)
    return grad.reshape(features.shape), direction, perturbed


def solution(mesh):
    return jax.shard_map(
        shards,
        mesh=mesh,
        in_specs=(P("lat", "lon", None), P("lat", "lon", None), P()),
        out_specs=(P("lat", "lon", None), P("lat", None), P("lat", None)),
        check_vma=False,
    )
```

time: 274 us -> 70.9 us (0.26)
  waiting for transfers between devices: 151 us -> 0 us
  Pallas kernels: 0 us -> 64.4 us
  matrix products: 59.8 us -> 0 us
  starting transfers between devices: 33.3 us -> 0 us
  between operations: 14.9 us -> 0.64 us
  other arithmetic: 8.16 us -> 0 us
    reduce_scatter x1 -> x0, waiting for transfers between devices: 139 us -> none  [shards(): lax.psum_scatter(local_grad, 'lat', scatter_dimension=0, tiled=True)]
    pallas_call x0 -> x1, Pallas kernels: none -> 64.4 us  [shards(): pl.pallas_call(kernel, name='ascent', out_shape=(jax.ShapeDtypeStruct((PO...]
    dot_general x27 -> x0, matrix products: 59.8 us -> none  [the longest x9 34.1 us: spread(): lax.dot_general(piece, kernel[t * channels:(t + 1) * channels], (((2,), (...]
    ppermute x8 -> x0, starting transfers between devices: 21.4 us -> none  [the longest x4 11.3 us: padded_2(): lax.ppermute(lax.slice_in_dim(block, block.shape[dim] - width, None, axis...]
    all_to_all x2 -> x0, starting transfers between devices: 11.8 us -> none  [from_everyone(): lax.all_to_all(jnp.broadcast_to(x[None], (size, *x.shape)), axis, 0, 0, t...]
    all_to_all x2 -> x0, waiting for transfers between devices: 9.65 us -> none  [from_everyone(): lax.all_to_all(jnp.broadcast_to(x[None], (size, *x.shape)), axis, 0, 0, t...]
    unnamed x12 -> x3, local copies, waits for them, and re-layouts: 0.54 us -> 5.67 us
    broadcast_in_dim x2 -> x0, local copies, waits for them, and re-layouts: 3.96 us -> none  [from_everyone(): jnp.broadcast_to(x[None], (size, *x.shape))]
  transfers between devices with their start and end apart: 11 -> 0, of which waited for: 5 -> 0; matrix products, arithmetic and copies ran while one was open for 16% -> 0% of each run, Pallas kernels for 0% -> 0%
where the time goes in v1:
time: 70.9 us; the launch traced here: 70.7 us
  Pallas kernels  64.4 us (91%)
  local copies, waits for them, and re-layouts  5.67 us (8%)
    pallas_call x1, Pallas kernels, shards(): pl.pallas_call(kernel, name='ascent', out_shape=(jax.ShapeDtypeStruct((PO...  64.4 us
    unnamed x3, local copies, waits for them, and re-layouts  5.67 us

profile of v1, /device:TPU:1, one launch (start us, length us, event | category | flops | bytes accessed | tf_op | source)
XLA Modules:
  0.0 70.7 jit_solution(16733952818677127423)
XLA Ops:
  0.6 64.4 %ascent.1 = (bf16[1024,512]{1,0:T(8,128)(2,1)}, f32[144,512]{1,0:T(8,128)}, f32[144,512]{1,0:T(8,128)}) custom-call(bf16[1024,512]{1,0:T(8,128)(2,1)} %bitcast.4, bf16[1024,512]{1,0:T(8,128)(2,1)} %bitcast.5, bf16[4608,512]{1,0:T(8,128)(2,1)} %k_hbm.1), custom_call_target="tpu_custom_call" | custom-call | tf_op jit(solution)/shard_map/ascent/pallas_call | solution.py:392
  65.1 2.3 %copy.9 = bf16[16,64,512]{2,1,0:T(8,128)(2,1)} copy(bf16[16,64,512]{2,1,0:T(8,128)(2,1)} %bitcast.3) | data formatting | bytes 2097152
  67.3 1.7 %copy.10 = f32[144,512]{1,0:T(8,128)} copy(f32[144,512]{1,0:T(8,128)} %get-tuple-element.13) | data formatting | bytes 589824
  69.0 1.7 %copy.11 = f32[144,512]{1,0:T(8,128)} copy(f32[144,512]{1,0:T(8,128)} %get-tuple-element.14) | data formatting | bytes 589824
